TPU v7x, 32 devices: a whole 2x2x4 slice. The times are simulated.
32 devices in a mesh: img: 32 (over z, y, x, core).
Axes of the slice: x: 2, y: 2, z: 4, core: 2. Of those that a mesh axis runs over, the one named last changes fastest.
Arguments:
- queries: bfloat16 [12288, 1024], P('img'), may hold values from -10 to 10
- keys: bfloat16 [12288, 1024], P('img'), may hold values from -10 to 10
- values: bfloat16 [12288, 1024], P('img'), may hold values from -6 to 6
- out_grad: bfloat16 [12288, 1024], P('img'), may hold values from -6 to 6
- image_ids: int32 [12288], P('img'), may hold values from 0 to 31, never falling along the last dimension, each value on 1 to 1152 neighbouring positions
Outputs:
- attended: bfloat16 [12288, 1024], P('img')
- query_grad: bfloat16 [12288, 1024], P('img')
- key_grad: bfloat16 [12288, 1024], P('img')
- value_grad: bfloat16 [12288, 1024], P('img')
Inputs may be any that keep to these rules, and one draw needn't show every extreme that they name: `image_ids`: the regions of one image stand in consecutive rows, and ids rise along the rows; an image has 1 to 1152 regions, and some image has exactly 1152.
All inputs are finite; a program needn't handle non-finite values.
Results may differ from a plain program's by a relative error of at most 0.0069.
Values may be sent and summed in bfloat16 or wider, within the bound.
A program may use at most 192 MiB of HBM per device.

v0:
```python
import math

import jax
import jax.numpy as jnp
from jax import lax
from jax.experimental import pallas as pl
from jax.experimental.pallas import tpu as pltpu
from jax.sharding import PartitionSpec as P

HEAD_DIM = 64
REACH = 3
LANES = 128
TQ = 128
TK = 768
NO_TAG = 1 << 30


def dot_nt(a, b):
    return lax.dot_general(a, b, (((1,), (1,)), ((), ())), preferred_element_type=jnp.float32)


def dot_nn(a, b):
    return lax.dot_general(a, b, (((1,), (0,)), ((), ())), preferred_element_type=jnp.float32)


def attend_kernel(
    begins, ends, bounds, q_ref, k_ref, v_ref, g_ref, kt_ref, vt_ref, tag_cols, tag_rows,
    att_ref, dq_ref, dk_ref, dv_ref,
    s_buf, dp_buf, dk_acc, dv_acc, att_acc, dq_acc,
):
    dk_acc[...] = jnp.zeros_like(dk_acc)
    dv_acc[...] = jnp.zeros_like(dv_acc)
    low = lax.broadcasted_iota(jnp.int32, (TQ, LANES), 1) < HEAD_DIM
    scale = 1.0 / math.sqrt(HEAD_DIM)

    def one_tile(tile, carry):
        row0 = pl.multiple_of(tile * TQ, TQ)
        rows = pl.ds(row0, TQ)
        key_begin = begins[tile]
        key_end = ends[tile]
        key0 = (key_begin // LANES) * LANES
        steps = (key_end - key0 + TK - 1) // TK
        key0 = jnp.minimum(key0, k_ref.shape[0] - steps * TK)
        q = q_ref[rows, :].astype(jnp.float32) * scale
        g = g_ref[rows, :].astype(jnp.float32)
        q2 = jnp.concatenate(
            [jnp.where(low, q, 0.0), jnp.where(low, 0.0, q)], 0).astype(jnp.bfloat16)
        g2 = jnp.concatenate(
            [jnp.where(low, g, 0.0), jnp.where(low, 0.0, g)], 0).astype(jnp.bfloat16)
        q_tags = tag_rows[pl.ds(tile, 1), :]

        def score_step(j, peak):
            keys = pl.ds(pl.multiple_of(key0 + j * TK, LANES), TK)
            held = pl.ds(pl.multiple_of(j * TK, TK), TK)
            s = dot_nt(k_ref[keys, :], q2)
            same = tag_cols[keys, :] == q_tags
            s = jnp.concatenate(
                [jnp.where(same, s[:, :TQ], -1e30), jnp.where(same, s[:, TQ:], -1e30)], 1)
            s_buf[held, :] = s
            dp_buf[held, :] = dot_nt(v_ref[keys, :], g2)
            return jnp.maximum(peak, jnp.max(s.reshape(TK // 8, 8, 2 * TQ), 0))

        peak = lax.fori_loop(0, steps, score_step, jnp.full((8, 2 * TQ), -1e30, jnp.float32))
        peak = jnp.max(peak, 0, keepdims=True)

        def weight_step(j, sums):
            total, delta = sums
            held = pl.ds(pl.multiple_of(j * TK, TK), TK)
            w = jnp.exp(s_buf[held, :] - peak)
            s_buf[held, :] = w
            wd = w * dp_buf[held, :]
            total = total + jnp.sum(w.reshape(TK // 8, 8, 2 * TQ), 0)
            delta = delta + jnp.sum(wd.reshape(TK // 8, 8, 2 * TQ), 0)
            return total, delta

        zero = jnp.zeros((8, 2 * TQ), jnp.float32)
        total, delta = lax.fori_loop(0, steps, weight_step, (zero, zero))
        inverse = 1.0 / jnp.sum(total, 0, keepdims=True)
        delta = jnp.sum(delta, 0, keepdims=True) * inverse
        att_acc[...] = jnp.zeros_like(att_acc)
        dq_acc[...] = jnp.zeros_like(dq_acc)

        def grad_step(j, c):
            keys = pl.ds(pl.multiple_of(key0 + j * TK, LANES), TK)
            held = pl.ds(pl.multiple_of(j * TK, TK), TK)
            p = s_buf[held, :] * inverse
            ds = (p * (dp_buf[held, :] - delta)).astype(jnp.bfloat16)
            p = p.astype(jnp.bfloat16)
            att_acc[...] += dot_nn(vt_ref[:, keys], p)
            dq_acc[...] += dot_nn(kt_ref[:, keys], ds)
            dv_acc[keys, :] += dot_nn(p, g2)
            dk_acc[keys, :] += dot_nn(ds, q2)
            return c

        lax.fori_loop(0, steps, grad_step, 0)
        att = att_acc[...]
        dq = dq_acc[...] * scale
        top = lax.broadcasted_iota(jnp.int32, (LANES, TQ), 0) < HEAD_DIM
        att_ref[rows, :] = jnp.where(top, att[:, :TQ], att[:, TQ:]).T.astype(jnp.bfloat16)
        dq_ref[rows, :] = jnp.where(top, dq[:, :TQ], dq[:, TQ:]).T.astype(jnp.bfloat16)
        return carry

    lax.fori_loop(bounds[0], bounds[1], one_tile, 0)
    dk_ref[...] = dk_acc[...].astype(jnp.bfloat16)
    dv_ref[...] = dv_acc[...].astype(jnp.bfloat16)


def attend(q, k, v, g, tags, bounds, halo):
    width = q.shape[0]
    most = 2 * halo + TQ + 2 * TK
    span = -(-min(most, width + TK) // TK) * TK
    vmem = pl.BlockSpec(memory_space=pltpu.VMEM)
    smem = pl.BlockSpec(memory_space=pltpu.SMEM)
    begins = jnp.sum((tags[None, :] < tags[::TQ][:, None]).astype(jnp.int32), 1)
    ends = jnp.sum((tags[None, :] <= tags[TQ - 1 :: TQ][:, None]).astype(jnp.int32), 1)
    out = jax.ShapeDtypeStruct((width, LANES), jnp.bfloat16)
    return pl.pallas_call(
        attend_kernel,
        out_shape=(out,) * 4,
        in_specs=[smem] * 3 + [vmem] * 8,
        out_specs=(vmem,) * 4,
        scratch_shapes=[
            pltpu.VMEM((span, 2 * TQ), jnp.float32),
            pltpu.VMEM((span, 2 * TQ), jnp.float32),
            pltpu.VMEM((width, LANES), jnp.float32),
            pltpu.VMEM((width, LANES), jnp.float32),
            pltpu.VMEM((LANES, 2 * TQ), jnp.float32),
            pltpu.VMEM((LANES, 2 * TQ), jnp.float32),
        ],
        compiler_params=pltpu.CompilerParams(vmem_limit_bytes=56 * 1024 * 1024),
        cost_estimate=pl.CostEstimate(
            flops=60_000_000_000, bytes_accessed=12_000_000, transcendentals=8_000_000),
    )(begins, ends, bounds, q, k, v, g, k.T, v.T,
      jnp.broadcast_to(tags[:, None], (width, LANES)), tags.reshape(width // LANES, LANES))


MESH = pl.DeviceIdType.MESH


def greet(me, base, pos, team, up, down):
    barrier = pltpu.get_barrier_semaphore()
    for step in range(1, team):
        mate = base + lax.rem(pos + step, team)
        pl.semaphore_signal(barrier, inc=1, device_id=(mate,), device_id_type=MESH)
    pl.semaphore_signal(barrier, inc=1, device_id=(up,), device_id_type=MESH)
    pl.semaphore_signal(barrier, inc=1, device_id=(down,), device_id_type=MESH)
    pl.semaphore_wait(barrier, team + 1)


def place(count, team):
    me = lax.axis_index("img")
    pos = lax.rem(me, team)
    return me, me - pos, pos, lax.rem(me + team, count), lax.rem(me + count - team, count)


def remote(src, dst, send_sem, recv_sem, device):
    copy = pltpu.make_async_remote_copy(
        src_ref=src, dst_ref=dst, send_sem=send_sem, recv_sem=recv_sem,
        device_id=(device,), device_id_type=MESH)
    return copy


def lanes_of(pos):
    return pl.ds(pl.multiple_of(pos * LANES, LANES), LANES)


def gather_kernel(count, team, *refs):
    ins, outs = refs[:5], refs[5:10]
    send, recv, halo_send, halo_recv = refs[10:]
    me, base, pos, up, down = place(count, team)
    greet(me, base, pos, team, up, down)
    copies = []
    for t, (src, dst) in enumerate(zip(ins, outs)):
        rows = src.shape[0]
        mine = pl.ds(pl.multiple_of(pos * rows, 8), rows)
        for step in range(1, team):
            mate = lax.rem(pos + step, team)
            part = src if t == 0 else src.at[:, lanes_of(mate)]
            copy = remote(
                part, dst.at[mine, :], send.at[t, step], recv.at[t, step], base + mate)
            copy.start()
            copies.append(copy)
    for t, (src, dst) in enumerate(zip(ins, outs)):
        rows = src.shape[0]
        mine = pl.ds(pl.multiple_of(pos * rows, 8), rows)
        dst[mine, :] = src[...] if t == 0 else src[:, lanes_of(pos)]
    later = []
    for t, dst in enumerate(outs):
        rows = ins[t].shape[0]
        for copy in copies[t * (team - 1) : (t + 1) * (team - 1)]:
            copy.wait_recv()
        copy = remote(
            dst.at[pl.ds(0, REACH * rows), :], dst.at[pl.ds(team * rows, REACH * rows), :],
            halo_send.at[t], halo_recv.at[t], down)
        copy.start()
        later.append(copy)
        if t == 0:
            copy = remote(
                dst.at[pl.ds((team - 1) * rows, rows), :],
                dst.at[pl.ds((team + REACH) * rows, rows), :],
                halo_send.at[5], halo_recv.at[5], up)
            copy.start()
            later.append(copy)
    for copy in later:
        copy.wait()
    for copy in copies:
        copy.wait_send()


def gather(count, team, tags, arrays):
    rows = arrays[0].shape[0]
    vmem = pl.BlockSpec(memory_space=pltpu.VMEM)
    width = (team + REACH) * rows
    tag_rows = (team + REACH + 1) * tags.shape[0]
    return pl.pallas_call(
        lambda *refs: gather_kernel(count, team, *refs),
        out_shape=(jax.ShapeDtypeStruct((tag_rows, LANES), jnp.int32),)
        + (jax.ShapeDtypeStruct((width, LANES), jnp.bfloat16),) * 4,
        in_specs=[vmem] * 5,
        out_specs=(vmem,) * 5,
        scratch_shapes=[
            pltpu.SemaphoreType.DMA((5, team)),
            pltpu.SemaphoreType.DMA((5, team)),
            pltpu.SemaphoreType.DMA((6,)),
            pltpu.SemaphoreType.DMA((6,)),
        ],
        compiler_params=pltpu.CompilerParams(collective_id=0, has_side_effects=True),
        name="gather",
    )(tags, *arrays)


def scatter_kernel(count, team, *refs):
    below, ins, outs = refs[0], refs[1:5], refs[5:9]
    far, staged, send, recv, halo_send, halo_recv = refs[9:]
    me, base, pos, up, down = place(count, team)
    rows = outs[0].shape[0]
    halo = REACH * rows
    greet(me, base, pos, team, up, down)
    halos = []
    for t, src in enumerate(ins):
        copy = remote(
            src.at[pl.ds(team * rows, halo), :], far.at[t], halo_send.at[t], halo_recv.at[t], up)
        copy.start()
        halos.append(copy)

    def block(t, step, early):
        mate = lax.rem(pos + step, team)
        at = pl.ds(pl.multiple_of(mate * rows, 16), rows) if early else pl.ds(
            pl.multiple_of(lax.rem(mate, REACH) * rows, 16), rows)
        src = ins[t].at[at, :] if early else staged.at[t, at, :]
        return remote(
            src, outs[t].at[:, lanes_of(pos)], send.at[t, step], recv.at[t, step], base + mate)

    for t in range(4):
        for step in range(1, team):
            @pl.when(lax.rem(pos + step, team) >= REACH)
            def _():
                block(t, step, True).start()

    for t in range(4):
        halos[t].wait_recv()

        def choose(i, c):
            at = pl.ds(pl.multiple_of(i * LANES, LANES), LANES)
            mixed = jnp.where(
                below[at, :] > 0, far[t, at, :].astype(jnp.float32),
                ins[t][at, :].astype(jnp.float32))
            staged[t, at, :] = mixed.astype(jnp.bfloat16)
            return c

        lax.fori_loop(0, halo // LANES, choose, 0)
        for step in range(1, team):
            @pl.when(lax.rem(pos + step, team) < REACH)
            def _():
                block(t, step, False).start()

    @pl.when(pos < REACH)
    def _():
        for t in range(4):
            at = pl.ds(pl.multiple_of(lax.rem(pos, REACH) * rows, 16), rows)
            outs[t][:, lanes_of(pos)] = staged[t, at, :]

    @pl.when(pos >= REACH)
    def _():
        for t in range(4):
            outs[t][:, lanes_of(pos)] = ins[t][pl.ds(pl.multiple_of(pos * rows, 16), rows), :]

    for t in range(4):
        for step in range(1, team):
            copy = block(t, step, True)
            copy.wait_recv()
            copy.wait_send()
        halos[t].wait_send()


def scatter(count, team, below, arrays):
    halo = below.shape[0]
    rows = halo // REACH
    vmem = pl.BlockSpec(memory_space=pltpu.VMEM)
    return pl.pallas_call(
        lambda *refs: scatter_kernel(count, team, *refs),
        out_shape=(jax.ShapeDtypeStruct((rows, team * LANES), jnp.bfloat16),) * 4,
        in_specs=[vmem] * 5,
        out_specs=(vmem,) * 4,
        scratch_shapes=[
            pltpu.VMEM((4, halo, LANES), jnp.bfloat16),
            pltpu.VMEM((4, halo, LANES), jnp.bfloat16),
            pltpu.SemaphoreType.DMA((4, team)),
            pltpu.SemaphoreType.DMA((4, team)),
            pltpu.SemaphoreType.DMA((4,)),
            pltpu.SemaphoreType.DMA((4,)),
        ],
        compiler_params=pltpu.CompilerParams(collective_id=1, has_side_effects=True),
        name="scatter",
    )(below, *arrays)


def shards(queries, keys, values, out_grad, image_ids):
    row_count, features = queries.shape
    count = lax.axis_size("img")
    team = features // LANES
    own = team * row_count
    halo = REACH * row_count
    width = own + halo

    tag_block = jnp.pad((image_ids + 1).reshape(row_count // LANES, LANES),
                        ((0, 8 - row_count // LANES), (0, 0)))
    tags, k, v, q, g = gather(count, team, tag_block, (keys, values, queries, out_grad))
    me = lax.axis_index("img")
    tags = tags.reshape(team + REACH + 1, 8, LANES)[:, : row_count // LANES].reshape(-1)
    before = jnp.where(me < team, 0, tags[-1])
    window = jnp.where((me >= count - team) & (jnp.arange(width) >= own), NO_TAG, tags[:width])
    first = jnp.sum((window == before).astype(jnp.int32))
    last = jnp.sum((window <= window[own - 1]).astype(jnp.int32))
    bounds = jnp.stack([first // TQ, (last + TQ - 1) // TQ]).astype(jnp.int32)
    results = attend(q, k, v, g, window, bounds, halo)
    below = jnp.broadcast_to((window[:halo] == before).astype(jnp.int32)[:, None], (halo, LANES))
    return scatter(count, team, below, results)


def solution(mesh):
    in_specs = (P("img", None), P("img", None), P("img", None), P("img", None), P("img"))
    out_specs = (P("img", None), P("img", None), P("img", None), P("img", None))
    return jax.shard_map(shards, mesh=mesh, in_specs=in_specs, out_specs=out_specs, check_vma=False)
```

profile of v0, /device:TPU:1, one launch (start us, length us, event | category | flops | bytes accessed | tf_op | source)
XLA Modules:
  0.0 191.4 jit_solution(11517807649433074820)
XLA Ops:
  0.6 0.7 add_bitcast_fusion
  1.3 0.6 pad.4.refs_0_
  1.9 52.0 %gather.1 = (s32[96,128]{1,0:T(8,128)}, bf16[4224,128]{1,0:T(8,128)(2,1)}, bf16[4224,128]{1,0:T(8,128)(2,1)}, bf16[4224,128]{1,0:T(8,128)(2,1)}, bf16[4224,128]{1,0:T(8,128)(2,1)}) custom-call(s32[8,128]{1,0:T(8,128)} %pad.4.refs_0_, bf16[384,1024]{1,0:T(8,128)(2,1)} %refs_1_.1, bf16[384,1024]{1,0:T(8,128)(2,1)} %refs_2_.1, bf16[384,1024]{1,0:T(8,128)(2,1)} %refs_3_.1, ...), custom_call_target="tpu_custom_call" | custom-call | tf_op jit(solution)/shard_map/gather/pallas_call | solution.py:215
  53.9 0.8 slice.36
  54.7 0.6 slice.40
  55.3 0.8 slice.38
  56.1 0.6 slice.39
  57.3 2.1 %convert_reduce_fusion.3 = (s32[]{:T(128)}, s32[]{:T(128)}) fusion(s32[]{:T(128)S(6)} %select_n.32, pred[]{:T(512)S(6)} %ge.28, s32[12,8,128]{2,1,0:T(8,128)} %bitcast.13, s32[]{:T(128)} %bitcast.4), kind=kLoop, calls=%fused_computation.3 | loop fusion | flops 54910 | bytes 16913 | tf_op jit(solution)/shard_map/reduce_sum | solution.py:333
  62.7 0.6 pad_add_fusion.bounds
  63.3 0.1 slice.32
  63.4 0.1 slice.33
  63.5 0.9 convert_reduce_fusion
  64.4 0.0 copy-start
  64.4 2.9 %broadcast_in_dim.27.tag_cols = s32[4224,128]{1,0:T(8,128)} broadcast(s32[4224]{0:T(1024)S(1)} %fusion.5), dimensions={0} | broadcast | bytes 2179584 | tf_op jit(solution)/shard_map/broadcast_in_dim | solution.py:134
  67.4 0.6 fusion.3.tag_rows
  68.0 0.0 copy-done
  68.0 0.0 copy-start.1
  68.0 1.7 copy.11
  69.7 0.0 copy-done.1
  69.7 1.6 copy.12
  71.3 60.1 %shard_map.84 = (bf16[4224,128]{1,0:T(8,128)(2,1)}, bf16[4224,128]{1,0:T(8,128)(2,1)}, bf16[4224,128]{1,0:T(8,128)(2,1)}, bf16[4224,128]{1,0:T(8,128)(2,1)}) custom-call(s32[33]{0:T(128)} %get-tuple-element.25.begins, s32[33]{0:T(128)} %get-tuple-element.24.ends, s32[2]{0:T(128)} %pad_add_fusion.bounds, bf16[4224,128]{1,0:T(8,128)(2,1)} %get-tuple-element.14.q_ref, ...), custom_call_target="tpu_custom_call" | custom-call | flops 60000002048 | bytes 12000000 | tf_op jit(solution)/shard_map/pallas_call | solution.py:117
  131.5 1.0 broadcast_in_dim.13.refs_0_
  132.5 53.0 %scatter.1 = (bf16[384,1024]{1,0:T(8,128)(2,1)}, bf16[384,1024]{1,0:T(8,128)(2,1)}, bf16[384,1024]{1,0:T(8,128)(2,1)}, bf16[384,1024]{1,0:T(8,128)(2,1)}) custom-call(s32[1152,128]{1,0:T(8,128)} %broadcast_in_dim.13.refs_0_, bf16[4224,128]{1,0:T(8,128)(2,1)} %get-tuple-element.18.refs_1_, bf16[4224,128]{1,0:T(8,128)(2,1)} %get-tuple-element.19.refs_2_, ...), custom_call_target="tpu_custom_call" | custom-call | tf_op jit(solution)/shard_map/scatter/pallas_call | solution.py:300
  185.5 0.0 copy-start.4
  185.6 2.1 %copy.17 = bf16[384,1024]{1,0:T(8,128)(2,1)} copy(bf16[384,1024]{1,0:T(8,128)(2,1)} %get-tuple-element.30) | data formatting | bytes 1572864
  187.7 0.0 copy-done.4
  187.7 0.0 copy-start.3
  187.7 0.9 copy.18
  188.6 0.5 copy-done.3
  189.1 0.0 copy-start.2
  189.1 0.9 copy.19
  190.0 0.5 copy-done.2
  190.5 0.9 copy.20
  (5 shorter events, 0.0 us)
Async XLA Ops:
  64.4 3.6 %copy-start = (bf16[4224,128]{1,0:T(8,128)(2,1)S(1)}, bf16[4224,128]{1,0:T(8,128)(2,1)}, u32[]{:S(2)}) copy-start(bf16[4224,128]{1,0:T(8,128)(2,1)} %get-tuple-element.15.k_ref) | copy-start | bytes 3244036
  68.0 1.7 copy-start.1
  185.5 2.1 %copy-start.4 = (bf16[384,1024]{1,0:T(8,128)(2,1)S(1)}, bf16[384,1024]{1,0:T(8,128)(2,1)}, u32[]{:S(2)}) copy-start(bf16[384,1024]{1,0:T(8,128)(2,1)} %get-tuple-element.31) | copy-start | bytes 2359300
  187.7 1.4 copy-start.3
  189.1 1.4 copy-start.2
where the time goes:
time: 190 us; the launch traced here: 191 us
  Pallas kernels  165 us (87%)
  local copies, waits for them, and re-layouts  16.8 us (9%)
  other arithmetic  4.85 us (3%)
  between operations  4.61 us (2%)
    pallas_call x1, Pallas kernels, attend(): pl.pallas_call(attend_kernel, out_shape=(out,) * 4, in_specs=[smem] * 3 +...  60.1 us
    pallas_call x1, Pallas kernels, scatter(): pl.pallas_call(lambda *refs: scatter_kernel(count, team, *refs), out_shap...  53 us
    pallas_call x1, Pallas kernels, gather(): pl.pallas_call(lambda *refs: gather_kernel(count, team, *refs), out_shape...  52 us
    unnamed x14, local copies, waits for them, and re-layouts  5.86 us

commit v1 on v0

v1 whole, which is shorter than its diff:
```python
import math

import jax
import jax.numpy as jnp
from jax import lax
from jax.experimental import pallas as pl
from jax.experimental.pallas import tpu as pltpu
from jax.sharding import PartitionSpec as P

HEAD_DIM = 64
REACH = 3
LANES = 128
TAG_ROWS = 8
TQ = 256
TK = 256
SB = 64
NO_TAG = 1 << 30
OUTSIDE = -1e30
MESH = pl.DeviceIdType.MESH
VMEM = pl.BlockSpec(memory_space=pltpu.VMEM)
ANY = pl.BlockSpec(memory_space=pl.ANY)
HBM = pl.BlockSpec(memory_space=pltpu.HBM)


def dot_nt(a, b):
    return lax.dot_general(a, b, (((1,), (1,)), ((), ())), preferred_element_type=jnp.float32)


def dot_nn(a, b):
    return lax.dot_general(a, b, (((1,), (0,)), ((), ())), preferred_element_type=jnp.float32)


def bf16(*shape):
    return jax.ShapeDtypeStruct(shape, jnp.bfloat16)


def f32(*shape):
    return jax.ShapeDtypeStruct(shape, jnp.float32)


def greet(base, pos, team, up, down):
    barrier = pltpu.get_barrier_semaphore()
    for step in range(1, team):
        mate = base + lax.rem(pos + step, team)
        pl.semaphore_signal(barrier, inc=1, device_id=(mate,), device_id_type=MESH)
    pl.semaphore_signal(barrier, inc=1, device_id=(up,), device_id_type=MESH)
    pl.semaphore_signal(barrier, inc=1, device_id=(down,), device_id_type=MESH)
    pl.semaphore_wait(barrier, team + 1)


def place(count, team):
    me = lax.axis_index("img")
    pos = lax.rem(me, team)
    return me, me - pos, pos, lax.rem(me + team, count), lax.rem(me + count - team, count)


def remote(src, dst, send_sem, recv_sem, device):
    return pltpu.make_async_remote_copy(
        src_ref=src, dst_ref=dst, send_sem=send_sem, recv_sem=recv_sem,
        device_id=(device,), device_id_type=MESH)


def lanes_of(pos):
    return pl.ds(pl.multiple_of(pos * LANES, LANES), LANES)


def gather_kernel(count, team, *refs):
    ins, outs = refs[:5], refs[5:10]
    kt, vt, qt, marks = refs[10:14]
    send, recv, halo_send, halo_recv, local = refs[14:]
    tags, kw, vw, _, _ = outs
    me, base, pos, up, down = place(count, team)
    above = me + team < count
    below = me >= team
    greet(base, pos, team, up, down)
    rows = [src.shape[0] for src in ins]
    halos = [REACH * r if t < 3 else 0 for t, r in enumerate(rows)]
    copies, own = [], []
    for t, (src, dst) in enumerate(zip(ins, outs)):
        mine = pl.ds(pl.multiple_of(halos[t] + pos * rows[t], 8), rows[t])
        for step in range(1, team):
            mate = lax.rem(pos + step, team)
            part = src if t == 0 else src.at[:, lanes_of(mate)]
            copy = remote(part, dst.at[mine, :], send.at[t, step], recv.at[t, step], base + mate)
            copy.start()
            copies.append(copy)
        part = src if t == 0 else src.at[:, lanes_of(pos)]
        copy = pltpu.make_async_copy(part, dst.at[mine, :], local.at[t])
        copy.start()
        own.append(copy)

    def halo_copies(t):
        dst, r, h = outs[t], rows[t], halos[t]
        down_copy = remote(dst.at[pl.ds(h, h), :], dst.at[pl.ds(h + team * r, h), :],
                           halo_send.at[t, 0], halo_recv.at[t, 0], down)
        up_copy = remote(dst.at[pl.ds(team * r, h), :], dst.at[pl.ds(0, h), :],
                         halo_send.at[t, 1], halo_recv.at[t, 1], up)
        return down_copy, up_copy

    def arrived(t):
        for copy in copies[t * (team - 1) : (t + 1) * (team - 1)]:
            copy.wait_recv()
        own[t].wait()

    def forward(t):
        down_copy, up_copy = halo_copies(t)
        pl.when(below)(down_copy.start)
        pl.when(above)(up_copy.start)

    def halo_arrived(t):
        down_copy, up_copy = halo_copies(t)
        pl.when(above)(down_copy.wait_recv)
        pl.when(below)(up_copy.wait_recv)

    def flip(src, dst, start, size):
        def step(i, c):
            for u in range(3):
                at = pl.ds(pl.multiple_of(start + (3 * i + u) * LANES, LANES), LANES)
                dst[:, at] = src[at, :].astype(jnp.float32).T.astype(jnp.bfloat16)
            return c
        lax.fori_loop(0, size // LANES // 3, step, 0)

    span = kw.shape[0]
    halo = halos[1]
    inner = span - 2 * halo

    @pl.when(jnp.logical_not(below))
    def _():
        kw[:halo, :] = jnp.zeros((halo, LANES), jnp.bfloat16)
        vw[:halo, :] = jnp.zeros((halo, LANES), jnp.bfloat16)
        used = lax.rem(lax.broadcasted_iota(jnp.int32, (halos[0], LANES), 0), TAG_ROWS)
        tags[: halos[0], :] = jnp.where(used < rows[1] // LANES, 0, NO_TAG)

    @pl.when(jnp.logical_not(above))
    def _():
        kw[halo + inner :, :] = jnp.zeros((halo, LANES), jnp.bfloat16)
        vw[halo + inner :, :] = jnp.zeros((halo, LANES), jnp.bfloat16)
        tags[halos[0] + team * rows[0] :, :] = jnp.full((halos[0], LANES), NO_TAG, jnp.int32)

    arrived(0)
    forward(0)
    arrived(1)
    forward(1)
    halo_arrived(0)
    ids = lax.broadcasted_iota(jnp.int32, (LANES, LANES), 0)

    def mark(i, c):
        for u in range(rows[1] // LANES):
            at = pl.ds(pl.multiple_of(i * rows[1] + u * LANES, LANES), LANES)
            tag = tags[pl.ds(i * TAG_ROWS + u, 1), :]
            outside = (tag <= 0) | (tag >= NO_TAG)
            hit = jnp.where((ids == lax.rem(tag, LANES)) | outside, 1.0, 0.0)
            marks[at, :] = hit.T.astype(jnp.bfloat16)
        return c

    lax.fori_loop(0, span // rows[1], mark, 0)
    flip(kw, kt, halo, inner)
    arrived(2)
    forward(2)
    halo_arrived(1)
    flip(kw, kt, 0, halo)
    flip(kw, kt, halo + inner, halo)
    flip(vw, vt, halo, inner)
    arrived(3)
    flip(outs[3], qt, 0, inner)
    halo_arrived(2)
    flip(vw, vt, 0, halo)
    flip(vw, vt, halo + inner, halo)
    arrived(4)
    for t in range(3):
        down_copy, up_copy = halo_copies(t)
        pl.when(below)(down_copy.wait_send)
        pl.when(above)(up_copy.wait_send)
    for copy in copies:
        copy.wait_send()


def gather(count, team, tags, arrays):
    rows = arrays[0].shape[0]
    span = (team + 2 * REACH) * rows
    return pl.pallas_call(
        lambda *refs: gather_kernel(count, team, *refs),
        out_shape=(
            jax.ShapeDtypeStruct(((team + 2 * REACH) * TAG_ROWS, LANES), jnp.int32),
            bf16(span, LANES), bf16(span, LANES), bf16(team * rows, LANES), bf16(team * rows, LANES),
            bf16(LANES, span), bf16(LANES, span), bf16(LANES, team * rows), bf16(span, LANES)),
        in_specs=[VMEM] + [HBM] * 4,
        out_specs=(VMEM,) * 9,
        scratch_shapes=[
            pltpu.SemaphoreType.DMA((5, team)),
            pltpu.SemaphoreType.DMA((5, team)),
            pltpu.SemaphoreType.DMA((3, 2)),
            pltpu.SemaphoreType.DMA((3, 2)),
            pltpu.SemaphoreType.DMA((5,)),
        ],
        compiler_params=pltpu.CompilerParams(
            collective_id=0, has_side_effects=True, vmem_limit_bytes=16 * 1024 * 1024),
        name="gather",
    )(tags, *arrays)


def attend_kernel(team, rows, *refs):
    tags, kw, vw, qw, gw, kt, vt, qt, marks = refs[:9]
    att_ref, dq_ref, dk_own, dv_own, dk_before, dk_after, dv_before, dv_after = refs[9:17]
    (s_buf, dp_buf, w_buf, p_buf, ds_buf, tops, sums, deltas, dk, dv, att_acc, dq_acc,
     qs, gs, qd, begins, ends) = refs[17:]
    halo = REACH * rows
    own = team * rows
    span = own + 2 * halo
    scale = 1.0 / math.sqrt(HEAD_DIM)
    low = lax.broadcasted_iota(jnp.int32, (TQ, LANES), 1) < HEAD_DIM
    ids = lax.broadcasted_iota(jnp.int32, (LANES, LANES), 0)
    tiles = own // TQ

    def tag_row(row):
        return (row // rows + REACH) * TAG_ROWS + row % rows // LANES

    for tile in range(tiles):
        first = tags[tag_row(tile * TQ) : tag_row(tile * TQ) + 1, :1]
        at = tag_row(tile * TQ + TQ - 1)
        final = tags[at : at + 1, LANES - 1 :]
        every = tags[...]
        begins[tile] = jnp.sum((every < first).astype(jnp.int32))
        ends[tile] = jnp.sum((every <= final).astype(jnp.int32))

    dk[...] = jnp.zeros_like(dk)
    dv[...] = jnp.zeros_like(dv)

    def one_tile(tile, carry):
        row0 = pl.multiple_of(tile * TQ, TQ)
        rows_here = pl.ds(row0, TQ)
        key0 = (begins[tile] // LANES) * LANES
        steps = (ends[tile] - key0 + TK - 1) // TK
        key0 = jnp.minimum(key0, span - steps * TK)

        q = qw[rows_here, :].astype(jnp.float32) * scale
        g = gw[rows_here, :].astype(jnp.float32)
        qd[:TQ, :] = jnp.where(low, q, 0.0).astype(jnp.bfloat16)
        qd[TQ:, :] = jnp.where(low, 0.0, q).astype(jnp.bfloat16)
        gs[:TQ, :] = jnp.where(low, g, 0.0).astype(jnp.bfloat16)
        gs[TQ:, :] = jnp.where(low, 0.0, g).astype(jnp.bfloat16)
        across = (qt[:, rows_here].astype(jnp.float32) * scale).astype(jnp.bfloat16)
        nothing = jnp.zeros((HEAD_DIM, TQ), jnp.bfloat16)
        qs[:HEAD_DIM, :TQ] = across[:HEAD_DIM]
        qs[HEAD_DIM:LANES, :TQ] = nothing
        qs[:HEAD_DIM, TQ:] = nothing
        qs[HEAD_DIM:LANES, TQ:] = across[HEAD_DIM:]
        for u in range(TQ // LANES):
            strip = tile * (TQ // LANES) + u
            per = rows // LANES
            tag = tags[pl.ds((strip // per + REACH) * TAG_ROWS + lax.rem(strip, per), 1), :]
            apart = jnp.where(ids == lax.rem(tag, LANES), 0.0, OUTSIDE).astype(jnp.bfloat16)
            qs[LANES:, u * LANES : (u + 1) * LANES] = apart
            qs[LANES:, TQ + u * LANES : TQ + (u + 1) * LANES] = apart

        def at_keys(j):
            return pl.ds(pl.multiple_of(key0 + j * TK, LANES), TK)

        def held(j):
            return pl.ds(pl.multiple_of(j * TK, TK), TK)

        def scores(j):
            keys = at_keys(j)
            s_buf[held(j), :] = dot_nn(jnp.concatenate([kw[keys, :], marks[keys, :]], 1), qs[...])
            dp_buf[held(j), :] = dot_nt(vw[keys, :], gs[...])

        def weights(j, top):
            for b in range(TK // SB):
                here = pl.ds(pl.multiple_of(j * TK + b * SB, SB), SB)
                at = pl.ds(pl.multiple_of((j * (TK // SB) + b) * 8, 8), 8)
                s = s_buf[here, :].reshape(SB // 8, 8, 2 * TQ)
                most = jnp.max(s, 0)
                w = jnp.exp(s - most[None])
                w_buf[here, :] = w.reshape(SB, 2 * TQ)
                sums[at, :] = jnp.sum(w, 0)
                deltas[at, :] = jnp.sum(w * dp_buf[here, :].reshape(SB // 8, 8, 2 * TQ), 0)
                tops[at, :] = most
                top = jnp.maximum(top, most)
            return top

        def score_step(j, top):
            scores(j)
            return weights(j, top)

        top = lax.fori_loop(0, steps, score_step, jnp.full((8, 2 * TQ), -3e38, jnp.float32))
        top = jnp.max(top, 0, keepdims=True)

        def total_step(j, carry):
            total, delta = carry
            for b in range(TK // SB):
                at = pl.ds(pl.multiple_of((j * (TK // SB) + b) * 8, 8), 8)
                factor = jnp.exp(tops[at, :] - top)
                tops[at, :] = factor
                total = total + factor * sums[at, :]
                delta = delta + factor * deltas[at, :]
            return total, delta

        none = jnp.zeros((8, 2 * TQ), jnp.float32)
        total, delta = lax.fori_loop(0, steps, total_step, (none, none))
        inverse = 1.0 / jnp.sum(total, 0, keepdims=True)
        delta = jnp.sum(delta, 0, keepdims=True) * inverse
        att_acc[...] = jnp.zeros_like(att_acc)
        dq_acc[...] = jnp.zeros_like(dq_acc)

        def probs(j):
            for b in range(TK // SB):
                here = pl.ds(pl.multiple_of(j * TK + b * SB, SB), SB)
                at = pl.ds(pl.multiple_of((j * (TK // SB) + b) * 8, 8), 8)
                factor = tops[at, :] * inverse
                p = w_buf[here, :].reshape(SB // 8, 8, 2 * TQ) * factor[None]
                p = p.reshape(SB, 2 * TQ)
                p_buf[here, :] = p.astype(jnp.bfloat16)
                ds_buf[here, :] = (p * (dp_buf[here, :] - delta)).astype(jnp.bfloat16)

        def grads(j):
            keys = at_keys(j)
            p = p_buf[held(j), :]
            ds = ds_buf[held(j), :]
            for half in (0, 1):
                dims = slice(half * HEAD_DIM, (half + 1) * HEAD_DIM)
                cols = slice(half * TQ, (half + 1) * TQ)
                att_acc[dims, :] += dot_nn(vt[dims, keys], p[:, cols])
                dq_acc[dims, :] += dot_nn(kt[dims, keys], ds[:, cols])
            dk[keys, :] += dot_nn(ds, qd[...])
            dv[keys, :] += dot_nn(p, gs[...])

        def grad_step(j, c):
            probs(j)
            grads(j)
            return c

        lax.fori_loop(0, steps, grad_step, 0)
        att_ref[rows_here, :] = att_acc[...].T.astype(jnp.bfloat16)
        dq_ref[rows_here, :] = (dq_acc[...].T * scale).astype(jnp.bfloat16)
        return carry

    lax.fori_loop(0, tiles, one_tile, 0)
    for acc, mine, before, after in ((dk, dk_own, dk_before, dk_after),
                                     (dv, dv_own, dv_before, dv_after)):
        mine[...] = acc[halo : halo + own, :]
        before[...] = acc[:halo, :].astype(jnp.bfloat16)
        after[...] = acc[halo + own :, :].astype(jnp.bfloat16)


def attend(team, rows, args):
    halo = REACH * rows
    own = team * rows
    span = own + 2 * halo
    held = -(-min(2 * halo + TQ + LANES + TK, span + TK) // TK) * TK
    f = jnp.float32
    scratch = [
        pltpu.VMEM((held, 2 * TQ), f),
        pltpu.VMEM((held, 2 * TQ), f),
        pltpu.VMEM((held, 2 * TQ), f),
        pltpu.VMEM((held, 2 * TQ), jnp.bfloat16),
        pltpu.VMEM((held, 2 * TQ), jnp.bfloat16),
        pltpu.VMEM((held // SB * 8, 2 * TQ), f),
        pltpu.VMEM((held // SB * 8, 2 * TQ), f),
        pltpu.VMEM((held // SB * 8, 2 * TQ), f),
        pltpu.VMEM((span, LANES), f),
        pltpu.VMEM((span, LANES), f),
        pltpu.VMEM((LANES, TQ), f),
        pltpu.VMEM((LANES, TQ), f),
        pltpu.VMEM((2 * LANES, 2 * TQ), jnp.bfloat16),
        pltpu.VMEM((2 * TQ, LANES), jnp.bfloat16),
        pltpu.VMEM((2 * TQ, LANES), jnp.bfloat16),
        pltpu.SMEM((own // TQ,), jnp.int32),
        pltpu.SMEM((own // TQ,), jnp.int32),
    ]
    outs = (bf16(own, LANES), bf16(own, LANES), f32(own, LANES), f32(own, LANES)) + (
        bf16(halo, LANES),) * 4
    return pl.pallas_call(
        lambda *refs: attend_kernel(team, rows, *refs),
        name="attend",
        out_shape=outs,
        in_specs=[VMEM] * len(args),
        out_specs=(VMEM,) * len(outs),
        scratch_shapes=scratch,
        compiler_params=pltpu.CompilerParams(vmem_limit_bytes=40 * 1024 * 1024),
        cost_estimate=pl.CostEstimate(
            flops=60_000_000_000, bytes_accessed=12_000_000, transcendentals=8_000_000),
    )(*args)


def scatter_kernel(count, team, *refs):
    att, dq, dk_own, dv_own, dk_before, dk_after, dv_before, dv_after = refs[:8]
    outs, (above_in, below_in, staged, send, recv, halo_send, halo_recv, local) = refs[8:12], refs[12:]
    me, base, pos, up, down = place(count, team)
    above = me + team < count
    below = me >= team
    rows = outs[0].shape[0]
    halo = REACH * rows
    own = team * rows
    greet(base, pos, team, up, down)

    def halo_copies(t):
        before, after = ((dk_before, dk_after), (dv_before, dv_after))[t]
        return (remote(before, above_in.at[t], halo_send.at[t, 0], halo_recv.at[t, 0], down),
                remote(after, below_in.at[t], halo_send.at[t, 1], halo_recv.at[t, 1], up))

    for t in range(2):
        down_copy, up_copy = halo_copies(t)
        pl.when(below)(down_copy.start)
        pl.when(above)(up_copy.start)
    copies = []

    def spread(t, src):
        for step in range(1, team):
            mate = lax.rem(pos + step, team)
            part = src.at[pl.ds(pl.multiple_of(mate * rows, 16), rows), :]
            copy = remote(part, outs[t].at[:, lanes_of(pos)], send.at[t, step], recv.at[t, step],
                          base + mate)
            copy.start()
            copies.append(copy)
        part = src.at[pl.ds(pl.multiple_of(pos * rows, 16), rows), :]
        copy = pltpu.make_async_copy(part, outs[t].at[:, lanes_of(pos)], local.at[t])
        copy.start()
        return copy

    mine = [spread(0, att), spread(1, dq)]
    for t, src in enumerate((dk_own, dv_own)):
        down_copy, up_copy = halo_copies(t)
        dst = staged.at[t]
        dst[halo : own - halo, :] = src[halo : own - halo, :].astype(jnp.bfloat16)

        @pl.when(above)
        def _():
            down_copy.wait_recv()
            dst[own - halo :, :] = (src[own - halo :, :] + above_in[t].astype(jnp.float32)
                                    ).astype(jnp.bfloat16)

        @pl.when(jnp.logical_not(above))
        def _():
            dst[own - halo :, :] = src[own - halo :, :].astype(jnp.bfloat16)

        @pl.when(below)
        def _():
            up_copy.wait_recv()
            dst[:halo, :] = (src[:halo, :] + below_in[t].astype(jnp.float32)).astype(jnp.bfloat16)

        @pl.when(jnp.logical_not(below))
        def _():
            dst[:halo, :] = src[:halo, :].astype(jnp.bfloat16)

        mine.append(spread(2 + t, dst))
    for copy in mine:
        copy.wait()
    for copy in copies:
        copy.wait_recv()
        copy.wait_send()
    for t in range(2):
        down_copy, up_copy = halo_copies(t)
        pl.when(below)(down_copy.wait_send)
        pl.when(above)(up_copy.wait_send)


def scatter(count, team, rows, arrays):
    halo = REACH * rows
    return pl.pallas_call(
        lambda *refs: scatter_kernel(count, team, *refs),
        out_shape=(bf16(rows, team * LANES),) * 4,
        in_specs=[VMEM] * 8,
        out_specs=(VMEM,) * 4,
        scratch_shapes=[
            pltpu.VMEM((2, halo, LANES), jnp.bfloat16),
            pltpu.VMEM((2, halo, LANES), jnp.bfloat16),
            pltpu.VMEM((2, team * rows, LANES), jnp.bfloat16),
            pltpu.SemaphoreType.DMA((4, team)),
            pltpu.SemaphoreType.DMA((4, team)),
            pltpu.SemaphoreType.DMA((2, 2)),
            pltpu.SemaphoreType.DMA((2, 2)),
            pltpu.SemaphoreType.DMA((4,)),
        ],
        compiler_params=pltpu.CompilerParams(
            collective_id=1, has_side_effects=True, vmem_limit_bytes=20 * 1024 * 1024),
        name="scatter",
    )(*arrays)


def settle(arrays):
    def kernel(*refs):
        ins, outs, sems = refs[:4], refs[4:8], refs[8]
        copies = [pltpu.make_async_copy(a, b, sems.at[i]) for i, (a, b) in enumerate(zip(ins, outs))]
        for copy in copies:
            copy.start()
        for copy in copies:
            copy.wait()

    return pl.pallas_call(
        kernel,
        name="settle",
        out_shape=tuple(jax.ShapeDtypeStruct(a.shape, a.dtype) for a in arrays),
        in_specs=[VMEM] * 4,
        out_specs=(HBM,) * 4,
        scratch_shapes=[pltpu.SemaphoreType.DMA((4,))],
        compiler_params=pltpu.CompilerParams(vmem_limit_bytes=4 * 1024 * 1024),
    )(*arrays)


def shards(queries, keys, values, out_grad, image_ids):
    rows, features = queries.shape
    count = lax.axis_size("img")
    team = features // LANES
    tags = jnp.pad((image_ids + 1).reshape(rows // LANES, LANES),
                   ((0, TAG_ROWS - rows // LANES), (0, 0)), constant_values=NO_TAG)
    gathered = gather(count, team, tags, (keys, values, queries, out_grad))
    results = attend(team, rows, gathered)
    attended, query_grad, key_grad, value_grad = scatter(count, team, rows, results)
    return settle((attended, query_grad, key_grad, value_grad))


def solution(mesh):
    in_specs = (P("img", None), P("img", None), P("img", None), P("img", None), P("img"))
    out_specs = (P("img", None), P("img", None), P("img", None), P("img", None))
    return jax.shard_map(shards, mesh=mesh, in_specs=in_specs, out_specs=out_specs, check_vma=False)
```

time: 190 us -> 143 us (0.75)
  Pallas kernels: 165 us -> 138 us
  local copies, waits for them, and re-layouts: 16.8 us -> 5.94 us
  other arithmetic: 4.85 us -> 0.68 us
  between operations: 4.61 us -> 0.65 us
    pallas_call x1, Pallas kernels: 53 us -> 37.9 us  [scatter(): pl.pallas_call(lambda *refs: scatter_kernel(count, team, *refs), out_shap...]
    pallas_call x1, Pallas kernels: 52 us -> 41.4 us  [gather(): pl.pallas_call(lambda *refs: gather_kernel(count, team, *refs), out_shape...]
    broadcast_in_dim x2 -> x0, local copies, waits for them, and re-layouts: 3.97 us -> none  [the longest x1 2.94 us: attend(): jnp.broadcast_to(tags[:, None], (width, LANES))]
    pallas_call x2 -> x0, local copies, waits for them, and re-layouts: 3.33 us -> none  [gather(): pl.pallas_call(lambda *refs: gather_kernel(count, team, *refs), out_shape...]
    slice x8 -> x0, local copies, waits for them, and re-layouts: 3.01 us -> none  [the longest x3 0.82 us: shards(): tags[:width]]
    reduce_sum x2 -> x0, other arithmetic: 2.96 us -> none  [the longest x1 2.1 us: shards(): first = jnp.sum((window == before).astype(jnp.int32))]
    pallas_call x1 -> x2, Pallas kernels: 60.1 us -> 58.6 us  [the longest x1 56.9 us: attend(): pl.pallas_call(lambda *refs: attend_kernel(team, rows, *refs), name='atte...]
    unnamed x14 -> x10, local copies, waits for them, and re-layouts: 5.86 us -> 5.94 us
where the time goes in v1:
time: 143 us; the launch traced here: 145 us
  Pallas kernels  138 us (97%)
  local copies, waits for them, and re-layouts  5.94 us (4%)
    pallas_call x1, Pallas kernels, attend(): pl.pallas_call(lambda *refs: attend_kernel(team, rows, *refs), name='atte...  56.9 us
    pallas_call x1, Pallas kernels, gather(): pl.pallas_call(lambda *refs: gather_kernel(count, team, *refs), out_shape...  41.4 us
    pallas_call x1, Pallas kernels, scatter(): pl.pallas_call(lambda *refs: scatter_kernel(count, team, *refs), out_shap...  37.9 us
    unnamed x10, local copies, waits for them, and re-layouts  5.94 us

profile of v1, /device:TPU:1, one launch (start us, length us, event | category | flops | bytes accessed | tf_op | source)
XLA Modules:
  0.0 145.3 jit_solution(11941164104430021993)
XLA Ops:
  0.6 0.7 add_bitcast_fusion
  1.3 0.0 copy-start.1
  1.3 1.1 copy-done.1
  2.5 0.0 copy-start.2
  2.5 1.1 copy-done.2
  3.6 0.0 copy-start.3
  3.6 1.1 copy-done.3
  4.7 0.0 copy-start.4
  4.7 1.1 copy-done.4
  5.9 41.4 %gather.1 = (s32[112,128]{1,0:T(8,128)S(1)}, bf16[5376,128]{1,0:T(8,128)(2,1)S(1)}, bf16[5376,128]{1,0:T(8,128)(2,1)S(1)}, bf16[3072,128]{1,0:T(8,128)(2,1)S(1)}...) custom-call(s32[8,128]{1,0:T(8,128)S(1)} %pad.4.refs_0_, ...), custom_call_target="tpu_custom_call" | custom-call | tf_op jit(solution)/shard_map/gather/pallas_call | solution.py:181
  47.3 56.9 %attend.1 = (bf16[3072,128]{1,0:T(8,128)(2,1)S(1)}, bf16[3072,128]{1,0:T(8,128)(2,1)S(1)}, f32[3072,128]{1,0:T(8,128)S(1)}, f32[3072,128]{1,0:T(8,128)}, bf16[11...) custom-call(s32[112,128]{1,0:T(8,128)S(1)} %get-tuple-element.25.ref, ...), custom_call_target="tpu_custom_call" | custom-call | flops 60000002048 | bytes 12000000 | tf_op jit(solution)/shard_map/attend/pallas_call | solution.py:372
  104.2 0.0 copy-start
  104.2 1.4 copy-done
  105.6 37.9 %scatter.1 = (bf16[384,1024]{1,0:T(8,128)(2,1)S(1)}, bf16[384,1024]{1,0:T(8,128)(2,1)S(1)}, bf16[384,1024]{1,0:T(8,128)(2,1)S(1)}, bf16[384,1024]{1,0:T(8,128)(2,1)S(1)}) custom-call(bf16[3072,128]{1,0:T(8,128)(2,1)S(1)} %get-tuple-element.34.refs_0_, bf16[3072,128]{1,0:T(8,128)(2,1)S(1)} %get-tuple-element.35.refs_1_, ...), custom_call_target="tpu_custom_call" | custom-call | tf_op jit(solution)/shard_map/scatter/pallas_call | solution.py:459
  143.6 1.7 %settle.1 = (bf16[384,1024]{1,0:T(8,128)(2,1)}, bf16[384,1024]{1,0:T(8,128)(2,1)}, bf16[384,1024]{1,0:T(8,128)(2,1)}, bf16[384,1024]{1,0:T(8,128)(2,1)}) custom-call(bf16[384,1024]{1,0:T(8,128)(2,1)S(1)} %get-tuple-element.42.refs_0_, bf16[384,1024]{1,0:T(8,128)(2,1)S(1)} %get-tuple-element.43.refs_1_, bf16[384,1024]{1,0:T(8,128)(2,1)S(1)} %get-tuple-element.44.refs_2_, ...), custom_call_target="tpu_custom_call" | custom-call | tf_op jit(solution)/shard_map/settle/pallas_call | solution.py:489
  (1 shorter events, 0.0 us)
Async XLA Ops:
  1.3 1.1 copy-start.1
  2.5 1.1 copy-start.2
  3.6 1.1 copy-start.3
  4.7 1.1 copy-start.4
  104.2 1.4 copy-start

commit v2 on v1

--- a/solution.py
+++ b/solution.py
@@ -13,7 +13,8 @@
 TAG_ROWS = 8
 TQ = 256
 TK = 256
-SB = 64
+SB = 128
+WHOLE = 6
 NO_TAG = 1 << 30
 OUTSIDE = -1e30
 MESH = pl.DeviceIdType.MESH
@@ -253,36 +254,38 @@
             qs[LANES:, u * LANES : (u + 1) * LANES] = apart
             qs[LANES:, TQ + u * LANES : TQ + (u + 1) * LANES] = apart
 
-        def at_keys(j):
-            return pl.ds(pl.multiple_of(key0 + j * TK, LANES), TK)
-
-        def held(j):
-            return pl.ds(pl.multiple_of(j * TK, TK), TK)
-
-        def scores(j):
-            keys = at_keys(j)
-            s_buf[held(j), :] = dot_nn(jnp.concatenate([kw[keys, :], marks[keys, :]], 1), qs[...])
-            dp_buf[held(j), :] = dot_nt(vw[keys, :], gs[...])
+        def scores(j, many):
+            keys = pl.ds(pl.multiple_of(key0 + j * TK, LANES), many * TK)
+            here = pl.ds(pl.multiple_of(j * TK, TK), many * TK)
+            s_buf[here, :] = dot_nn(jnp.concatenate([kw[keys, :], marks[keys, :]], 1), qs[...])
+            dp_buf[here, :] = dot_nt(vw[keys, :], gs[...])
 
         def weights(j, top):
-            for b in range(TK // SB):
-                here = pl.ds(pl.multiple_of(j * TK + b * SB, SB), SB)
-                at = pl.ds(pl.multiple_of((j * (TK // SB) + b) * 8, 8), 8)
-                s = s_buf[here, :].reshape(SB // 8, 8, 2 * TQ)
-                most = jnp.max(s, 0)
-                w = jnp.exp(s - most[None])
-                w_buf[here, :] = w.reshape(SB, 2 * TQ)
-                sums[at, :] = jnp.sum(w, 0)
-                deltas[at, :] = jnp.sum(w * dp_buf[here, :].reshape(SB // 8, 8, 2 * TQ), 0)
-                tops[at, :] = most
-                top = jnp.maximum(top, most)
-            return top
-
-        def score_step(j, top):
-            scores(j)
-            return weights(j, top)
-
-        top = lax.fori_loop(0, steps, score_step, jnp.full((8, 2 * TQ), -3e38, jnp.float32))
+            here = pl.ds(pl.multiple_of(j * SB, SB), SB)
+            at = pl.ds(pl.multiple_of(j * 8, 8), 8)
+            s = s_buf[here, :].reshape(SB // 8, 8, 2 * TQ)
+            most = jnp.max(s, 0)
+            w = jnp.exp(s - most[None])
+            w_buf[here, :] = w.reshape(SB, 2 * TQ)
+            sums[at, :] = jnp.sum(w, 0)
+            deltas[at, :] = jnp.sum(w * dp_buf[here, :].reshape(SB // 8, 8, 2 * TQ), 0)
+            tops[at, :] = most
+            return jnp.maximum(top, most)
+
+        def sweep(body):
+            def whole_step(j, c):
+                body(WHOLE * j, WHOLE)
+                return c
+
+            lax.fori_loop(0, steps // WHOLE, whole_step, 0)
+            for rest in range(1, WHOLE):
+                @pl.when(lax.rem(steps, WHOLE) == rest)
+                def _():
+                    body(steps - rest, rest)
+
+        sweep(scores)
+        parts = steps * (TK // SB)
+        top = lax.fori_loop(0, parts, weights, jnp.full((8, 2 * TQ), -3e38, jnp.float32))
         top = jnp.max(top, 0, keepdims=True)
 
         def total_step(j, carry):
@@ -302,34 +305,30 @@
         att_acc[...] = jnp.zeros_like(att_acc)
         dq_acc[...] = jnp.zeros_like(dq_acc)
 
-        def probs(j):
-            for b in range(TK // SB):
-                here = pl.ds(pl.multiple_of(j * TK + b * SB, SB), SB)
-                at = pl.ds(pl.multiple_of((j * (TK // SB) + b) * 8, 8), 8)
-                factor = tops[at, :] * inverse
-                p = w_buf[here, :].reshape(SB // 8, 8, 2 * TQ) * factor[None]
-                p = p.reshape(SB, 2 * TQ)
-                p_buf[here, :] = p.astype(jnp.bfloat16)
-                ds_buf[here, :] = (p * (dp_buf[here, :] - delta)).astype(jnp.bfloat16)
-
-        def grads(j):
-            keys = at_keys(j)
-            p = p_buf[held(j), :]
-            ds = ds_buf[held(j), :]
+        def probs(j, c):
+            here = pl.ds(pl.multiple_of(j * SB, SB), SB)
+            factor = tops[pl.ds(pl.multiple_of(j * 8, 8), 8), :] * inverse
+            p = w_buf[here, :].reshape(SB // 8, 8, 2 * TQ) * factor[None]
+            p = p.reshape(SB, 2 * TQ)
+            p_buf[here, :] = p.astype(jnp.bfloat16)
+            ds_buf[here, :] = (p * (dp_buf[here, :] - delta)).astype(jnp.bfloat16)
+            return c
+
+        def grads(j, many):
+            keys = pl.ds(pl.multiple_of(key0 + j * TK, LANES), many * TK)
+            here = pl.ds(pl.multiple_of(j * TK, TK), many * TK)
+            p = p_buf[here, :]
+            ds = ds_buf[here, :]
+            dk[keys, :] += dot_nn(ds, qd[...])
+            dv[keys, :] += dot_nn(p, gs[...])
             for half in (0, 1):
                 dims = slice(half * HEAD_DIM, (half + 1) * HEAD_DIM)
                 cols = slice(half * TQ, (half + 1) * TQ)
-                att_acc[dims, :] += dot_nn(vt[dims, keys], p[:, cols])
-                dq_acc[dims, :] += dot_nn(kt[dims, keys], ds[:, cols])
-            dk[keys, :] += dot_nn(ds, qd[...])
-            dv[keys, :] += dot_nn(p, gs[...])
-
-        def grad_step(j, c):
-            probs(j)
-            grads(j)
-            return c
-
-        lax.fori_loop(0, steps, grad_step, 0)
+                att_acc[dims, :] += dot_nn(vt[dims, keys], p_buf[here, cols])
+                dq_acc[dims, :] += dot_nn(kt[dims, keys], ds_buf[here, cols])
+
+        lax.fori_loop(0, parts, probs, 0)
+        sweep(grads)
         att_ref[rows_here, :] = att_acc[...].T.astype(jnp.bfloat16)
         dq_ref[rows_here, :] = (dq_acc[...].T * scale).astype(jnp.bfloat16)
         return carry
@@ -376,7 +375,7 @@
         in_specs=[VMEM] * len(args),
         out_specs=(VMEM,) * len(outs),
         scratch_shapes=scratch,
-        compiler_params=pltpu.CompilerParams(vmem_limit_bytes=40 * 1024 * 1024),
+        compiler_params=pltpu.CompilerParams(vmem_limit_bytes=35 * 1024 * 1024),
         cost_estimate=pl.CostEstimate(
             flops=60_000_000_000, bytes_accessed=12_000_000, transcendentals=8_000_000),
     )(*args)

time: 143 us -> 134 us (0.937); the launches traced: 145 us -> 133 us
  Pallas kernels: 138 us -> 127 us
    pallas_call x1, Pallas kernels: 56.9 us -> 46 us  [attend(): pl.pallas_call(lambda *refs: attend_kernel(team, rows, *refs), name='atte...]
    unnamed x10 -> x8, local copies, waits for them, and re-layouts: 5.94 us -> 4.53 us
where the time goes in v2:
time: 134 us; the launch traced here: 133 us
  Pallas kernels  127 us (95%)
  local copies, waits for them, and re-layouts  4.54 us (3%)
    pallas_call x1, Pallas kernels, attend(): pl.pallas_call(lambda *refs: attend_kernel(team, rows, *refs), name='atte...  46 us
    pallas_call x1, Pallas kernels, gather(): pl.pallas_call(lambda *refs: gather_kernel(count, team, *refs), out_shape...  41.4 us
    pallas_call x1, Pallas kernels, scatter(): pl.pallas_call(lambda *refs: scatter_kernel(count, team, *refs), out_shap...  38 us
    unnamed x8, local copies, waits for them, and re-layouts  4.53 us

profile of v2, /device:TPU:1, one launch (start us, length us, event | category | flops | bytes accessed | tf_op | source)
XLA Modules:
  0.0 133.0 jit_solution(7339081547741608432)
XLA Ops:
  0.6 0.7 add_bitcast_fusion
  1.3 0.0 copy-start
  1.3 1.1 copy-done
  2.5 0.0 copy-start.1
  2.5 1.1 copy-done.1
  3.6 0.0 copy-start.2
  3.6 1.1 copy-done.2
  4.7 0.0 copy-start.3
  4.7 1.1 copy-done.3
  5.9 41.4 %gather.1 = (s32[112,128]{1,0:T(8,128)S(1)}, bf16[5376,128]{1,0:T(8,128)(2,1)S(1)}, bf16[5376,128]{1,0:T(8,128)(2,1)S(1)}, bf16[3072,128]{1,0:T(8,128)(2,1)S(1)}...) custom-call(s32[8,128]{1,0:T(8,128)S(1)} %pad.4.refs_0_, ...), custom_call_target="tpu_custom_call" | custom-call | tf_op jit(solution)/shard_map/gather/pallas_call | solution.py:182
  47.3 46.0 %attend.1 = (bf16[3072,128]{1,0:T(8,128)(2,1)S(1)}, bf16[3072,128]{1,0:T(8,128)(2,1)S(1)}, f32[3072,128]{1,0:T(8,128)S(1)}, f32[3072,128]{1,0:T(8,128)S(1)}, bf1...) custom-call(s32[112,128]{1,0:T(8,128)S(1)} %get-tuple-element.25.ref, ...), custom_call_target="tpu_custom_call" | custom-call | flops 60000002048 | bytes 12000000 | tf_op jit(solution)/shard_map/attend/pallas_call | solution.py:371
  93.3 38.0 %scatter.1 = (bf16[384,1024]{1,0:T(8,128)(2,1)S(1)}, bf16[384,1024]{1,0:T(8,128)(2,1)S(1)}, bf16[384,1024]{1,0:T(8,128)(2,1)S(1)}, bf16[384,1024]{1,0:T(8,128)(2,1)S(1)}) custom-call(bf16[3072,128]{1,0:T(8,128)(2,1)S(1)} %get-tuple-element.34.refs_0_, bf16[3072,128]{1,0:T(8,128)(2,1)S(1)} %get-tuple-element.35.refs_1_, ...), custom_call_target="tpu_custom_call" | custom-call | tf_op jit(solution)/shard_map/scatter/pallas_call | solution.py:458
  131.3 1.7 %settle.1 = (bf16[384,1024]{1,0:T(8,128)(2,1)}, bf16[384,1024]{1,0:T(8,128)(2,1)}, bf16[384,1024]{1,0:T(8,128)(2,1)}, bf16[384,1024]{1,0:T(8,128)(2,1)}) custom-call(bf16[384,1024]{1,0:T(8,128)(2,1)S(1)} %get-tuple-element.42.refs_0_, bf16[384,1024]{1,0:T(8,128)(2,1)S(1)} %get-tuple-element.43.refs_1_, bf16[384,1024]{1,0:T(8,128)(2,1)S(1)} %get-tuple-element.44.refs_2_, ...), custom_call_target="tpu_custom_call" | custom-call | tf_op jit(solution)/shard_map/settle/pallas_call | solution.py:488
  (1 shorter events, 0.0 us)
Async XLA Ops:
  1.3 1.1 copy-start
  2.5 1.1 copy-start.1
  3.6 1.1 copy-start.2
  4.7 1.1 copy-start.3

commit v3 on v2

--- a/solution.py
+++ b/solution.py
@@ -185,7 +185,7 @@
             jax.ShapeDtypeStruct(((team + 2 * REACH) * TAG_ROWS, LANES), jnp.int32),
             bf16(span, LANES), bf16(span, LANES), bf16(team * rows, LANES), bf16(team * rows, LANES),
             bf16(LANES, span), bf16(LANES, span), bf16(LANES, team * rows), bf16(span, LANES)),
-        in_specs=[VMEM] + [HBM] * 4,
+        in_specs=[VMEM] * 5,
         out_specs=(VMEM,) * 9,
         scratch_shapes=[
             pltpu.SemaphoreType.DMA((5, team)),
@@ -260,17 +260,22 @@
             s_buf[here, :] = dot_nn(jnp.concatenate([kw[keys, :], marks[keys, :]], 1), qs[...])
             dp_buf[here, :] = dot_nt(vw[keys, :], gs[...])
 
-        def weights(j, top):
-            here = pl.ds(pl.multiple_of(j * SB, SB), SB)
-            at = pl.ds(pl.multiple_of(j * 8, 8), 8)
-            s = s_buf[here, :].reshape(SB // 8, 8, 2 * TQ)
-            most = jnp.max(s, 0)
-            w = jnp.exp(s - most[None])
-            w_buf[here, :] = w.reshape(SB, 2 * TQ)
-            sums[at, :] = jnp.sum(w, 0)
-            deltas[at, :] = jnp.sum(w * dp_buf[here, :].reshape(SB // 8, 8, 2 * TQ), 0)
-            tops[at, :] = most
-            return jnp.maximum(top, most)
+        def weights(j, many):
+            for u in range(many * TK // SB):
+                here = pl.ds(pl.multiple_of(j * TK + u * SB, SB), SB)
+                at = pl.ds(pl.multiple_of(j * (TK // SB * 8) + u * 8, 8), 8)
+                s = s_buf[here, :].reshape(SB // 8, 8, 2 * TQ)
+                most = jnp.max(s, 0)
+                w = jnp.exp(s - most[None])
+                w_buf[here, :] = w.reshape(SB, 2 * TQ)
+                sums[at, :] = jnp.sum(w, 0)
+                deltas[at, :] = jnp.sum(w * dp_buf[here, :].reshape(SB // 8, 8, 2 * TQ), 0)
+                tops[at, :] = most
+
+        def score(j, many):
+            for u in range(many):
+                scores(j + u, 1)
+                weights(j + u, 1)
 
         def sweep(body):
             def whole_step(j, c):
@@ -283,9 +288,13 @@
                 def _():
                     body(steps - rest, rest)
 
-        sweep(scores)
+        sweep(score)
         parts = steps * (TK // SB)
-        top = lax.fori_loop(0, parts, weights, jnp.full((8, 2 * TQ), -3e38, jnp.float32))
+
+        def top_step(j, top):
+            return jnp.maximum(top, tops[pl.ds(pl.multiple_of(j * 8, 8), 8), :])
+
+        top = lax.fori_loop(0, parts, top_step, jnp.full((8, 2 * TQ), -3e38, jnp.float32))
         top = jnp.max(top, 0, keepdims=True)
 
         def total_step(j, carry):
@@ -476,7 +485,7 @@
     )(*arrays)
 
 
-def settle(arrays):
+def move(arrays, source, target, name, grant):
     def kernel(*refs):
         ins, outs, sems = refs[:4], refs[4:8], refs[8]
         copies = [pltpu.make_async_copy(a, b, sems.at[i]) for i, (a, b) in enumerate(zip(ins, outs))]
@@ -487,12 +496,12 @@
 
     return pl.pallas_call(
         kernel,
-        name="settle",
+        name=name,
         out_shape=tuple(jax.ShapeDtypeStruct(a.shape, a.dtype) for a in arrays),
-        in_specs=[VMEM] * 4,
-        out_specs=(HBM,) * 4,
+        in_specs=[source] * 4,
+        out_specs=(target,) * 4,
         scratch_shapes=[pltpu.SemaphoreType.DMA((4,))],
-        compiler_params=pltpu.CompilerParams(vmem_limit_bytes=4 * 1024 * 1024),
+        compiler_params=pltpu.CompilerParams(vmem_limit_bytes=grant),
     )(*arrays)
 
 
@@ -502,10 +511,11 @@
     team = features // LANES
     tags = jnp.pad((image_ids + 1).reshape(rows // LANES, LANES),
                    ((0, TAG_ROWS - rows // LANES), (0, 0)), constant_values=NO_TAG)
-    gathered = gather(count, team, tags, (keys, values, queries, out_grad))
+    arrays = move((keys, values, queries, out_grad), HBM, VMEM, "load", 53_200_000)
+    gathered = gather(count, team, tags, arrays)
     results = attend(team, rows, gathered)
     attended, query_grad, key_grad, value_grad = scatter(count, team, rows, results)
-    return settle((attended, query_grad, key_grad, value_grad))
+    return move((attended, query_grad, key_grad, value_grad), VMEM, HBM, "settle", 4 * 1024 * 1024)
 
 
 def solution(mesh):

time: 134 us -> 124 us (0.925); the launches traced: 133 us -> 125 us
  local copies, waits for them, and re-layouts: 4.54 us -> 0.01 us
  Pallas kernels: 127 us -> 124 us
    pallas_call x1, Pallas kernels: 46 us -> 37.3 us  [attend(): pl.pallas_call(lambda *refs: attend_kernel(team, rows, *refs), name='atte...]
    unnamed x8 -> x0, local copies, waits for them, and re-layouts: 4.53 us -> none
    pallas_call x1, Pallas kernels: 38 us -> 41.1 us  [scatter(): pl.pallas_call(lambda *refs: scatter_kernel(count, team, *refs), out_shap...]
    pallas_call x1 -> x2, Pallas kernels: 1.69 us -> 3.57 us  [move(): pl.pallas_call(kernel, name=name, out_shape=tuple((jax.ShapeDtypeStruct(a...]
where the time goes in v3:
time: 124 us; the launch traced here: 125 us
  Pallas kernels  124 us (100%)
    pallas_call x1, Pallas kernels, gather(): pl.pallas_call(lambda *refs: gather_kernel(count, team, *refs), out_shape...  41.5 us
    pallas_call x1, Pallas kernels, scatter(): pl.pallas_call(lambda *refs: scatter_kernel(count, team, *refs), out_shap...  41.1 us
    pallas_call x1, Pallas kernels, attend(): pl.pallas_call(lambda *refs: attend_kernel(team, rows, *refs), name='atte...  37.3 us
    pallas_call x2, Pallas kernels, move(): pl.pallas_call(kernel, name=name, out_shape=tuple((jax.ShapeDtypeStruct(a...  3.57 us

profile of v3, /device:TPU:1, one launch (start us, length us, event | category | flops | bytes accessed | tf_op | source)
XLA Modules:
  0.0 124.9 jit_solution(14098049436271007402)
XLA Ops:
  0.6 0.7 add_bitcast_fusion
  1.3 1.9 %load.1 = (bf16[384,1024]{1,0:T(8,128)(2,1)S(1)}, bf16[384,1024]{1,0:T(8,128)(2,1)S(1)}, bf16[384,1024]{1,0:T(8,128)(2,1)S(1)}, bf16[384,1024]{1,0:T(8,128)(2,1)S(1)}) custom-call(bf16[384,1024]{1,0:T(8,128)(2,1)} %refs_0_.1, bf16[384,1024]{1,0:T(8,128)(2,1)} %refs_1_.1, bf16[384,1024]{1,0:T(8,128)(2,1)} %refs_2_.1, bf16[384,1024]{1,0:T(8,128)(2,1)} %refs_3_.1), custom_call_target="tpu_custom_call" | custom-call | tf_op jit(solution)/shard_map/load/pallas_call | solution.py:497
  3.2 41.5 %gather.1 = (s32[112,128]{1,0:T(8,128)S(1)}, bf16[5376,128]{1,0:T(8,128)(2,1)S(1)}, bf16[5376,128]{1,0:T(8,128)(2,1)S(1)}, bf16[3072,128]{1,0:T(8,128)(2,1)S(1)}...) custom-call(s32[8,128]{1,0:T(8,128)S(1)} %pad.4.refs_0_, ...), custom_call_target="tpu_custom_call" | custom-call | tf_op jit(solution)/shard_map/gather/pallas_call | solution.py:182
  44.7 37.3 %attend.1 = (bf16[3072,128]{1,0:T(8,128)(2,1)S(1)}, bf16[3072,128]{1,0:T(8,128)(2,1)S(1)}, f32[3072,128]{1,0:T(8,128)S(1)}, f32[3072,128]{1,0:T(8,128)S(1)}, bf1...) custom-call(s32[112,128]{1,0:T(8,128)S(1)} %get-tuple-element.33.ref, ...), custom_call_target="tpu_custom_call" | custom-call | flops 60000002048 | bytes 12000000 | tf_op jit(solution)/shard_map/attend/pallas_call | solution.py:380
  82.0 41.1 %scatter.1 = (bf16[384,1024]{1,0:T(8,128)(2,1)S(1)}, bf16[384,1024]{1,0:T(8,128)(2,1)S(1)}, bf16[384,1024]{1,0:T(8,128)(2,1)S(1)}, bf16[384,1024]{1,0:T(8,128)(2,1)S(1)}) custom-call(bf16[3072,128]{1,0:T(8,128)(2,1)S(1)} %get-tuple-element.42.refs_0_, bf16[3072,128]{1,0:T(8,128)(2,1)S(1)} %get-tuple-element.43.refs_1_, ...), custom_call_target="tpu_custom_call" | custom-call | tf_op jit(solution)/shard_map/scatter/pallas_call | solution.py:467
  123.2 1.7 %settle.1 = (bf16[384,1024]{1,0:T(8,128)(2,1)}, bf16[384,1024]{1,0:T(8,128)(2,1)}, bf16[384,1024]{1,0:T(8,128)(2,1)}, bf16[384,1024]{1,0:T(8,128)(2,1)}) custom-call(bf16[384,1024]{1,0:T(8,128)(2,1)S(1)} %get-tuple-element.50.refs_0_, bf16[384,1024]{1,0:T(8,128)(2,1)S(1)} %get-tuple-element.51.refs_1_, bf16[384,1024]{1,0:T(8,128)(2,1)S(1)} %get-tuple-element.52.refs_2_, ...), custom_call_target="tpu_custom_call" | custom-call | tf_op jit(solution)/shard_map/settle/pallas_call | solution.py:497
  (1 shorter events, 0.0 us)

commit v4 on v3

--- a/solution.py
+++ b/solution.py
@@ -13,7 +13,7 @@
 TAG_ROWS = 8
 TQ = 256
 TK = 256
-SB = 128
+SB = 256
 WHOLE = 6
 NO_TAG = 1 << 30
 OUTSIDE = -1e30
@@ -204,7 +204,7 @@
     tags, kw, vw, qw, gw, kt, vt, qt, marks = refs[:9]
     att_ref, dq_ref, dk_own, dv_own, dk_before, dk_after, dv_before, dv_after = refs[9:17]
     (s_buf, dp_buf, w_buf, p_buf, ds_buf, tops, sums, deltas, dk, dv, att_acc, dq_acc,
-     qs, gs, qd, begins, ends) = refs[17:]
+     qs, gs, qd, peak, begins, ends) = refs[17:]
     halo = REACH * rows
     own = team * rows
     span = own + 2 * halo
@@ -271,6 +271,7 @@
                 sums[at, :] = jnp.sum(w, 0)
                 deltas[at, :] = jnp.sum(w * dp_buf[here, :].reshape(SB // 8, 8, 2 * TQ), 0)
                 tops[at, :] = most
+                peak[...] = jnp.maximum(peak[...], most)
 
         def score(j, many):
             for u in range(many):
@@ -288,19 +289,15 @@
                 def _():
                     body(steps - rest, rest)
 
+        peak[...] = jnp.full((8, 2 * TQ), -3e38, jnp.float32)
         sweep(score)
         parts = steps * (TK // SB)
-
-        def top_step(j, top):
-            return jnp.maximum(top, tops[pl.ds(pl.multiple_of(j * 8, 8), 8), :])
-
-        top = lax.fori_loop(0, parts, top_step, jnp.full((8, 2 * TQ), -3e38, jnp.float32))
-        top = jnp.max(top, 0, keepdims=True)
+        top = jnp.max(peak[...], 0, keepdims=True)
 
         def total_step(j, carry):
             total, delta = carry
-            for b in range(TK // SB):
-                at = pl.ds(pl.multiple_of((j * (TK // SB) + b) * 8, 8), 8)
+            for u in range(TK // SB):
+                at = pl.ds(pl.multiple_of(j * (TK // SB * 8) + u * 8, 8), 8)
                 factor = jnp.exp(tops[at, :] - top)
                 tops[at, :] = factor
                 total = total + factor * sums[at, :]
@@ -372,6 +369,7 @@
         pltpu.VMEM((2 * LANES, 2 * TQ), jnp.bfloat16),
         pltpu.VMEM((2 * TQ, LANES), jnp.bfloat16),
         pltpu.VMEM((2 * TQ, LANES), jnp.bfloat16),
+        pltpu.VMEM((8, 2 * TQ), f),
         pltpu.SMEM((own // TQ,), jnp.int32),
         pltpu.SMEM((own // TQ,), jnp.int32),
     ]

time: 124 us -> 124 us (level)
    pallas_call x1, Pallas kernels: 37.3 us -> 41.2 us  [attend(): pl.pallas_call(lambda *refs: attend_kernel(team, rows, *refs), name='atte...]
    pallas_call x1, Pallas kernels: 41.1 us -> 38 us  [scatter(): pl.pallas_call(lambda *refs: scatter_kernel(count, team, *refs), out_shap...]
where the time goes in v4:
time: 124 us; the launch traced here: 126 us
  Pallas kernels  124 us (100%)
    pallas_call x1, Pallas kernels, gather(): pl.pallas_call(lambda *refs: gather_kernel(count, team, *refs), out_shape...  41.5 us
    pallas_call x1, Pallas kernels, attend(): pl.pallas_call(lambda *refs: attend_kernel(team, rows, *refs), name='atte...  41.2 us
    pallas_call x1, Pallas kernels, scatter(): pl.pallas_call(lambda *refs: scatter_kernel(count, team, *refs), out_shap...  38 us
    pallas_call x2, Pallas kernels, move(): pl.pallas_call(kernel, name=name, out_shape=tuple((jax.ShapeDtypeStruct(a...  3.57 us

profile of v4, /device:TPU:1, one launch (start us, length us, event | category | flops | bytes accessed | tf_op | source)
XLA Modules:
  0.0 125.6 jit_solution(10266721531216197903)
XLA Ops:
  0.6 0.7 add_bitcast_fusion
  1.3 1.9 %load.1 = (bf16[384,1024]{1,0:T(8,128)(2,1)S(1)}, bf16[384,1024]{1,0:T(8,128)(2,1)S(1)}, bf16[384,1024]{1,0:T(8,128)(2,1)S(1)}, bf16[384,1024]{1,0:T(8,128)(2,1)S(1)}) custom-call(bf16[384,1024]{1,0:T(8,128)(2,1)} %refs_0_.1, bf16[384,1024]{1,0:T(8,128)(2,1)} %refs_1_.1, bf16[384,1024]{1,0:T(8,128)(2,1)} %refs_2_.1, bf16[384,1024]{1,0:T(8,128)(2,1)} %refs_3_.1), custom_call_target="tpu_custom_call" | custom-call | tf_op jit(solution)/shard_map/load/pallas_call | solution.py:495
  3.2 41.5 %gather.1 = (s32[112,128]{1,0:T(8,128)S(1)}, bf16[5376,128]{1,0:T(8,128)(2,1)S(1)}, bf16[5376,128]{1,0:T(8,128)(2,1)S(1)}, bf16[3072,128]{1,0:T(8,128)(2,1)S(1)}...) custom-call(s32[8,128]{1,0:T(8,128)S(1)} %pad.4.refs_0_, ...), custom_call_target="tpu_custom_call" | custom-call | tf_op jit(solution)/shard_map/gather/pallas_call | solution.py:182
  44.7 41.2 %attend.1 = (bf16[3072,128]{1,0:T(8,128)(2,1)S(1)}, bf16[3072,128]{1,0:T(8,128)(2,1)S(1)}, f32[3072,128]{1,0:T(8,128)S(1)}, f32[3072,128]{1,0:T(8,128)S(1)}, bf1...) custom-call(s32[112,128]{1,0:T(8,128)S(1)} %get-tuple-element.33.ref, ...), custom_call_target="tpu_custom_call" | custom-call | flops 60000002048 | bytes 12000000 | tf_op jit(solution)/shard_map/attend/pallas_call | solution.py:378
  85.9 38.0 %scatter.1 = (bf16[384,1024]{1,0:T(8,128)(2,1)S(1)}, bf16[384,1024]{1,0:T(8,128)(2,1)S(1)}, bf16[384,1024]{1,0:T(8,128)(2,1)S(1)}, bf16[384,1024]{1,0:T(8,128)(2,1)S(1)}) custom-call(bf16[3072,128]{1,0:T(8,128)(2,1)S(1)} %get-tuple-element.42.refs_0_, bf16[3072,128]{1,0:T(8,128)(2,1)S(1)} %get-tuple-element.43.refs_1_, ...), custom_call_target="tpu_custom_call" | custom-call | tf_op jit(solution)/shard_map/scatter/pallas_call | solution.py:465
  123.9 1.7 %settle.1 = (bf16[384,1024]{1,0:T(8,128)(2,1)}, bf16[384,1024]{1,0:T(8,128)(2,1)}, bf16[384,1024]{1,0:T(8,128)(2,1)}, bf16[384,1024]{1,0:T(8,128)(2,1)}) custom-call(bf16[384,1024]{1,0:T(8,128)(2,1)S(1)} %get-tuple-element.50.refs_0_, bf16[384,1024]{1,0:T(8,128)(2,1)S(1)} %get-tuple-element.51.refs_1_, bf16[384,1024]{1,0:T(8,128)(2,1)S(1)} %get-tuple-element.52.refs_2_, ...), custom_call_target="tpu_custom_call" | custom-call | tf_op jit(solution)/shard_map/settle/pallas_call | solution.py:495
  (1 shorter events, 0.0 us)

commit v5 on v4

--- a/solution.py
+++ b/solution.py
@@ -15,6 +15,7 @@
 TK = 256
 SB = 256
 WHOLE = 6
+SLICES = 4
 NO_TAG = 1 << 30
 OUTSIDE = -1e30
 MESH = pl.DeviceIdType.MESH
@@ -486,7 +487,12 @@
 def move(arrays, source, target, name, grant):
     def kernel(*refs):
         ins, outs, sems = refs[:4], refs[4:8], refs[8]
-        copies = [pltpu.make_async_copy(a, b, sems.at[i]) for i, (a, b) in enumerate(zip(ins, outs))]
+        copies = []
+        for i, (a, b) in enumerate(zip(ins, outs)):
+            part = a.shape[0] // SLICES
+            for j in range(SLICES):
+                at = pl.ds(j * part, part)
+                copies.append(pltpu.make_async_copy(a.at[at, :], b.at[at, :], sems.at[i, j]))
         for copy in copies:
             copy.start()
         for copy in copies:
@@ -498,7 +504,7 @@
         out_shape=tuple(jax.ShapeDtypeStruct(a.shape, a.dtype) for a in arrays),
         in_specs=[source] * 4,
         out_specs=(target,) * 4,
-        scratch_shapes=[pltpu.SemaphoreType.DMA((4,))],
+        scratch_shapes=[pltpu.SemaphoreType.DMA((4, SLICES))],
         compiler_params=pltpu.CompilerParams(vmem_limit_bytes=grant),
     )(*arrays)
 

time: 124 us -> 124 us (level); the launches traced: 126 us -> 124 us
    pallas_call x1, Pallas kernels: 41.2 us -> 38 us  [attend(): pl.pallas_call(lambda *refs: attend_kernel(team, rows, *refs), name='atte...]
    pallas_call x1, Pallas kernels: 38 us -> 39.4 us  [scatter(): pl.pallas_call(lambda *refs: scatter_kernel(count, team, *refs), out_shap...]
where the time goes in v5:
time: 124 us
  Pallas kernels  123 us (99%)
    pallas_call x1, Pallas kernels, gather(): pl.pallas_call(lambda *refs: gather_kernel(count, team, *refs), out_shape...  41.5 us
    pallas_call x1, Pallas kernels, scatter(): pl.pallas_call(lambda *refs: scatter_kernel(count, team, *refs), out_shap...  39.4 us
    pallas_call x1, Pallas kernels, attend(): pl.pallas_call(lambda *refs: attend_kernel(team, rows, *refs), name='atte...  38 us
    pallas_call x2, Pallas kernels, move(): pl.pallas_call(kernel, name=name, out_shape=tuple((jax.ShapeDtypeStruct(a...  3.85 us

profile of v5, /device:TPU:1, one launch (start us, length us, event | category | flops | bytes accessed | tf_op | source)
XLA Modules:
  0.0 124.1 jit_solution(16229584954693510716)
XLA Ops:
  0.6 0.7 add_bitcast_fusion
  1.3 2.1 %load.1 = (bf16[384,1024]{1,0:T(8,128)(2,1)S(1)}, bf16[384,1024]{1,0:T(8,128)(2,1)S(1)}, bf16[384,1024]{1,0:T(8,128)(2,1)S(1)}, bf16[384,1024]{1,0:T(8,128)(2,1)S(1)}) custom-call(bf16[384,1024]{1,0:T(8,128)(2,1)} %refs_0_.1, bf16[384,1024]{1,0:T(8,128)(2,1)} %refs_1_.1, bf16[384,1024]{1,0:T(8,128)(2,1)} %refs_2_.1, bf16[384,1024]{1,0:T(8,128)(2,1)} %refs_3_.1), custom_call_target="tpu_custom_call" | custom-call | tf_op jit(solution)/shard_map/load/pallas_call | solution.py:501
  3.4 41.5 %gather.1 = (s32[112,128]{1,0:T(8,128)S(1)}, bf16[5376,128]{1,0:T(8,128)(2,1)S(1)}, bf16[5376,128]{1,0:T(8,128)(2,1)S(1)}, bf16[3072,128]{1,0:T(8,128)(2,1)S(1)}...) custom-call(s32[8,128]{1,0:T(8,128)S(1)} %pad.4.refs_0_, ...), custom_call_target="tpu_custom_call" | custom-call | tf_op jit(solution)/shard_map/gather/pallas_call | solution.py:183
  44.9 38.0 %attend.1 = (bf16[3072,128]{1,0:T(8,128)(2,1)S(1)}, bf16[3072,128]{1,0:T(8,128)(2,1)S(1)}, f32[3072,128]{1,0:T(8,128)S(1)}, f32[3072,128]{1,0:T(8,128)S(1)}, bf1...) custom-call(s32[112,128]{1,0:T(8,128)S(1)} %get-tuple-element.33.ref, ...), custom_call_target="tpu_custom_call" | custom-call | flops 60000002048 | bytes 12000000 | tf_op jit(solution)/shard_map/attend/pallas_call | solution.py:379
  82.9 39.4 %scatter.1 = (bf16[384,1024]{1,0:T(8,128)(2,1)S(1)}, bf16[384,1024]{1,0:T(8,128)(2,1)S(1)}, bf16[384,1024]{1,0:T(8,128)(2,1)S(1)}, bf16[384,1024]{1,0:T(8,128)(2,1)S(1)}) custom-call(bf16[3072,128]{1,0:T(8,128)(2,1)S(1)} %get-tuple-element.42.refs_0_, bf16[3072,128]{1,0:T(8,128)(2,1)S(1)} %get-tuple-element.43.refs_1_, ...), custom_call_target="tpu_custom_call" | custom-call | tf_op jit(solution)/shard_map/scatter/pallas_call | solution.py:466
  122.3 1.8 %settle.1 = (bf16[384,1024]{1,0:T(8,128)(2,1)}, bf16[384,1024]{1,0:T(8,128)(2,1)}, bf16[384,1024]{1,0:T(8,128)(2,1)}, bf16[384,1024]{1,0:T(8,128)(2,1)}) custom-call(bf16[384,1024]{1,0:T(8,128)(2,1)S(1)} %get-tuple-element.50.refs_0_, bf16[384,1024]{1,0:T(8,128)(2,1)S(1)} %get-tuple-element.51.refs_1_, bf16[384,1024]{1,0:T(8,128)(2,1)S(1)} %get-tuple-element.52.refs_2_, ...), custom_call_target="tpu_custom_call" | custom-call | tf_op jit(solution)/shard_map/settle/pallas_call | solution.py:501
  (1 shorter events, 0.0 us)
